TPU v7x, 32 devices: a whole 2x2x4 slice. The times are simulated.
32 devices in a mesh: grp: 4 (over x, core), sub: 8 (over z, y).
Axes of the slice: x: 2, y: 2, z: 4, core: 2. Of those that a mesh axis runs over, the one named last changes fastest.
Arguments:
- snapshots: bfloat16 [2048, 2, 32, 128], P(None, None, ('grp', 'sub')), may hold values from -6 to 6
- steering: bfloat16 [32, 2, 128, 64], P(('grp', 'sub')), may hold values from -0.375 to 0.375
- combining: bfloat16 [32, 2, 64, 1024], P(('grp', 'sub')), may hold values from -0.09375 to 0.09375
- beam_list: int32 [1024], replicated, may hold values from 0 to 1023, each once
Outputs:
- beams_out: bfloat16 [2, 2048, 1024], P(None, ('grp', 'sub'))
Inputs may be any that keep to these rules, and one draw needn't show every extreme that they name: `beam_list`: each of the 1024 beams appears once.
All inputs are finite; a program needn't handle non-finite values.
Results may differ from a plain program's by a relative error of at most 0.0065.
Values may be sent and summed in bfloat16 or wider, within the bound.
A program may use at most 128 MiB of HBM per device.

v0:
```python
import jax
import jax.numpy as jnp
from jax import lax
from jax.sharding import PartitionSpec as P


def widen_block(portion):
    real_part = portion[:, 0]
    imag_part = portion[:, 1]
    top_rows = jnp.concatenate([real_part, imag_part], axis=-1)
    low_rows = jnp.concatenate([-imag_part, real_part], axis=-1)
    stacked = jnp.stack([top_rows, low_rows], axis=1)
    return stacked.reshape(portion.shape[0], 2 * portion.shape[2], 2 * portion.shape[3])


def shards(snapshots, steering, combining, beam_list):
    group_count = lax.axis_size("grp")
    sub_count = lax.axis_size("sub")
    snap_count = snapshots.shape[0]
    block_rows = snap_count // (group_count * sub_count)
    beam_count = combining.shape[3]
    sig_real = snapshots[:, 0, 0, :]
    sig_imag = snapshots[:, 1, 0, :]
    steer_real = steering[0, 0]
    steer_imag = steering[0, 1]
    upper_w = jnp.concatenate([steer_real, steer_imag], axis=1)
    lower_w = jnp.concatenate([-steer_imag, steer_real], axis=1)
    partial_value = (
        jnp.dot(sig_real, upper_w, preferred_element_type=jnp.float32)
        + jnp.dot(sig_imag, lower_w, preferred_element_type=jnp.float32)
    ).astype(jnp.bfloat16)
    ordered = jnp.take(combining, beam_list, axis=3)
    width = partial_value.shape[1]
    regrouped = lax.all_to_all(
        partial_value.reshape(group_count, sub_count, block_rows, width),
        "sub",
        split_axis=1,
        concat_axis=1,
        tiled=True,
    )
    running = jnp.einsum(
        "gurc,ucn->grn",
        regrouped,
        widen_block(lax.all_gather(ordered, "sub", axis=0, tiled=True)),
        preferred_element_type=jnp.float32,
    )
    summed = lax.psum_scatter(running, "grp", scatter_dimension=0, tiled=True)[0]
    shaped = summed.reshape(block_rows, 2, beam_count)
    return jnp.transpose(shaped, (1, 0, 2)).astype(jnp.bfloat16)


def solution(mesh):
    placed = (
        P(None, None, ("grp", "sub"), None),
        P(("grp", "sub"), None, None, None),
        P(("grp", "sub"), None, None, None),
        P(),
    )
    return jax.shard_map(
        shards, mesh=mesh, in_specs=placed, out_specs=P(None, ("grp", "sub"), None), check_vma=False
    )
```

profile of v0, /device:TPU:0, one launch (start us, length us, event | category | flops | bytes accessed | tf_op | source)
XLA Modules:
  0.0 125.9 jit_solution(6054358913419497896)
XLA Ops:
  6.5 0.0 copy-start.2
  6.5 0.0 copy-start.1
  6.5 0.0 all-gather.2.cloned.1.call-start
  6.5 0.8 fusion.9
  7.3 0.7 compare_and_fusion
  8.0 1.3 copy.37
  9.3 3.7 %gather_fusion = bf16[1024,2,64]{2,1,0:T(2,128)(2,1)S(1)} fusion(bf16[2,64,1024]{1,0,2:T(2,128)(2,1)S(1)} %bitcast.48, s32[1024]{0:T(1024)S(1)} %fusion.9), kind=kCustom, calls=%fused_computation | custom fusion | bytes 528384 | tf_op jit(solution)/shard_map/jit(_take)/gather | solution.py:32
  13.0 3.7 %broadcast_select_fusion = bf16[1,2,64,1024]{2,1,3,0:T(2,128)(2,1)S(1)} fusion(pred[1024]{0:T(1024)(128)(4,1)S(1)} %compare_and_fusion, bf16[1024,2,64]{2,1,0:T(2,128)(2,1)S(1)} %gather_fusion), kind=kLoop, calls=%fused_computation.10 | loop fusion | flops 131072 | bytes 525312 | tf_op jit(solution)/shard_map/jit(_take)/select_n | solution.py:32
  16.7 1.0 copy.38
  17.8 0.0 all-gather.2.cloned.1.call-update
  17.8 0.0 copy-done.2
  17.8 0.0 copy-done.1
  17.8 1.5 %fusion.14 = (bf16[2048,1,1,128]{3,1,2,0:T(2,128)(2,1)S(1)}, bf16[2048,1,1,128]{3,1,2,0:T(2,128)(2,1)S(1)}) fusion(bf16[2048,2,1,128]{3,1,2,0:T(2,128)(2,1)S(1)} %copy-done.1), kind=kLoop, calls=%fused_computation.30 | loop fusion | bytes 2097152 | tf_op jit(solution)/shard_map/slice | solution.py:23
  19.3 0.3 fusion.2
  19.6 0.3 fusion.1
  20.0 0.3 copy.35
  20.2 0.8 copy.36
  21.1 7.3 %all-to-all-start = ((bf16[4,8,64,128]{3,2,0,1:T(8,128)(2,1)}), bf16[4,8,64,128]{3,2,0,1:T(8,128)(2,1)S(1)}, u32[]{:S(2)}, u32[]{:S(2)}) async-start(bf16[4,8,64,128]{3,2,0,1:T(8,128)(2,1)} %copy.36), calls=%async_computation | async-start | bytes 1048576 | tf_op jit(solution)/shard_map/all_to_all | solution.py:34
  28.4 0.0 reduce-scatter.2.cloned.1.call-start
  28.4 48.6 %all-gather.2.cloned.1.call-done = bf16[8,2,64,1024]{3,2,1,0:T(8,128)(2,1)} async-done(((bf16[1,2,64,1024]{3,2,1,0:T(8,128)(2,1)}), bf16[8,2,64,1024]{3,2,1,0:T(8,128)(2,1)}) %all-gather.2.cloned.1.call-update) | async-done | bytes 2097168 | tf_op jit(solution)/shard_map/all_gather | solution.py:44
  77.1 0.0 copy-start
  77.1 1.9 %slice_bitcast_fusion = (bf16[8,64,1024]{2,1,0:T(8,128)(2,1)S(1)}, bf16[8,64,1024]{2,1,0:T(8,128)(2,1)S(1)}) fusion(bf16[8,2,64,1024]{3,2,1,0:T(8,128)(2,1)} %all-gather.2.cloned.1.call-done), kind=kLoop, calls=%fused_computation.8 | loop fusion | bytes 4194304 | tf_op jit(solution)/shard_map/squeeze | solution.py:9
  78.9 0.4 copy-done
  79.3 0.1 fusion.13
  79.4 0.4 maximum_bitcast_fusion
  79.8 0.4 pad_maximum_fusion
  80.2 2.3 %copy.41 = bf16[8,2,64,2048]{3,2,1,0:T(8,128)(2,1)} copy(bf16[8,2,64,2048]{3,2,0,1:T(8,128)(2,1)S(1)} %pad_maximum_fusion) | data formatting | bytes 8388608 | tf_op jit(solution)/shard_map/stack | solution.py:12
  82.5 0.0 all-to-all-done
  82.5 4.8 %convolution_bitcast_fusion = f32[4,64,2048]{2,1,0:T(8,128)} fusion(bf16[4,8,64,128]{3,2,0,1:T(8,128)(2,1)S(1)} %all-to-all-done, bf16[8,128,2048,1]{2,1,3,0:T(8,128)(2,1)} %bitcast.46), kind=kOutput, calls=%fused_computation.2 | convolution fusion | flops 1073741824 | bytes 6815744 | tf_op jit(solution)/shard_map/gurc,ucn->grn/dot_general | solution.py:41
  87.2 0.0 reduce-scatter.2.cloned.1.call-update
  87.3 29.8 %reduce-scatter.2.cloned.1.call-done = f32[1,64,2048]{2,1,0:T(8,128)} async-done(((f32[4,64,2048]{2,1,0:T(8,128)}), f32[1,64,2048]{2,1,0:T(8,128)}) %reduce-scatter.2.cloned.1.call-update) | async-done | bytes 524304 | tf_op jit(solution)/shard_map/reduce_scatter | solution.py:47
  117.1 1.1 convert_element_type.17
  118.2 0.2 convert_element_type.18
  118.3 0.8 copy.55
  (2 shorter events, 0.0 us)
Async XLA Ops:
  6.5 11.2 %copy-start.2 = (bf16[1,2,128,64]{2,3,1,0:T(8,128)(2,1)S(1)}, bf16[1,2,128,64]{2,3,1,0:T(8,128)(2,1)}, u32[]{:S(2)}) copy-start(bf16[1,2,128,64]{2,3,1,0:T(8,128)(2,1)} %param.5) | copy-start | bytes 98308
  6.5 11.3 %copy-start.1 = (bf16[2048,2,1,128]{3,1,2,0:T(2,128)(2,1)S(1)}, bf16[2048,2,1,128]{3,1,2,0:T(2,128)(2,1)}, u32[]{:S(2)}) copy-start(bf16[2048,2,1,128]{3,1,2,0:T(2,128)(2,1)} %param.4) | copy-start | bytes 3145732
  6.5 70.5 %all-gather.2.cloned.1.call-start = ((), (), s32[]{:S(2)}) async-start(), calls=%async_computation.2 | async-start | bytes 2359296 | tf_op jit(solution)/shard_map/all_gather | solution.py:44
  21.1 61.4 %all-to-all-start = ((bf16[4,8,64,128]{3,2,0,1:T(8,128)(2,1)}), bf16[4,8,64,128]{3,2,0,1:T(8,128)(2,1)S(1)}, u32[]{:S(2)}, u32[]{:S(2)}) async-start(bf16[4,8,64,128]{3,2,0,1:T(8,128)(2,1)} %copy.36), calls=%async_computation | async-start | bytes 1048576 | tf_op jit(solution)/shard_map/all_to_all | solution.py:34
  28.4 88.7 %reduce-scatter.2.cloned.1.call-start = ((), (), s32[]{:S(2)}) async-start(), calls=%async_computation.3 | async-start | bytes 2621440 | tf_op jit(solution)/shard_map/reduce_scatter | solution.py:47
  77.1 2.2 %copy-start = (bf16[8,2,64,1024]{3,2,1,0:T(8,128)(2,1)S(1)}, bf16[8,2,64,1024]{3,2,1,0:T(8,128)(2,1)}, u32[]{:S(2)}) copy-start(bf16[8,2,64,1024]{3,2,1,0:T(8,128)(2,1)} %all-gather.2.cloned.1.call-done) | copy-start | bytes 6291460
Sparse Core Ops, SparseCore 0:
  17.9 59.1 all-gather.1
  87.4 29.6 reduce-scatter.1
where the time goes:
time: 126 us
  waiting for transfers between devices  78.5 us (62%)
  local copies, waits for them, and re-layouts  14 us (11%)
  between operations  13.5 us (11%)
  starting transfers between devices  7.35 us (6%)
  other arithmetic  7.19 us (6%)
  matrix products  5.37 us (4%)
    all_gather x1, waiting for transfers between devices, shards(): lax.all_gather(ordered, 'sub', axis=0, tiled=True)  48.6 us
    reduce_scatter x1, waiting for transfers between devices, shards(): lax.psum_scatter(running, 'grp', scatter_dimension=0, tiled=True)[0]  29.8 us
    all_to_all x1, starting transfers between devices, shards(): lax.all_to_all(partial_value.reshape(group_count, sub_count, block_rows,...  7.31 us
    dot_general x1, matrix products, shards(): jnp.einsum('gurc,ucn->grn', regrouped, widen_block(lax.all_gather(ordered...  4.76 us
    select_n x1, other arithmetic, shards(): ordered = jnp.take(combining, beam_list, axis=3)  3.74 us
    gather x1, local copies, waits for them, and re-layouts, shards(): ordered = jnp.take(combining, beam_list, axis=3)  3.69 us
  transfers between devices with their start and end apart: 3, of which 2 were waited for; matrix products, arithmetic and copies ran while one was open for 7% of the time, Pallas kernels for 0%

commit v1 on v0

v1 whole, which is shorter than its diff:
```python
import functools

import jax
import jax.numpy as jnp
from jax import lax
from jax.experimental import pallas as pl
from jax.experimental.pallas import tpu as pltpu
from jax.sharding import PartitionSpec as P

MESH = pl.DeviceIdType.MESH
F32 = jnp.float32
BF16 = jnp.bfloat16


class Plan:
    def __init__(self, mesh, snap, width, beams):
        self.grp = mesh.shape["grp"]
        self.sub = mesh.shape["sub"]
        self.cores = 2 if self.grp % 2 == 0 else 1
        self.nx = self.grp // self.cores
        self.hi = self.grp if self.sub % self.grp == 0 else 1
        self.lo = self.sub // self.hi
        self.block = snap // (self.grp * self.sub)
        self.width = width
        self.beams = beams
        self.chunks = 4 if beams % 512 == 0 else 1
        self.cols = beams // self.chunks
        self.offsets = [(dx, dy) for dx in range(self.nx) for dy in range(self.lo)]
        self.slots = len(self.offsets) * self.cores


def beam_kernel(
    plan,
    x_ref,
    s_ref,
    w_ref,
    list_ref,
    out_ref,
    even_buf,
    odd_buf,
    pall,
    pbuf,
    lhs_buf,
    wbuf,
    own_buf,
    share_buf,
    got_buf,
    pick_buf,
    acc_buf,
    psend,
    precv,
    wsend,
    wrecv,
    ssend,
    srecv,
):
    cores, nx, lo, hi = plan.cores, plan.nx, plan.lo, plan.hi
    cols, width, block = plan.cols, plan.width, plan.block
    half = width // 2
    offsets = plan.offsets
    count = len(offsets)
    g = lax.axis_index("grp")
    s = lax.axis_index("sub")
    core, xi = lax.rem(g, cores), lax.div(g, cores)
    z, y = lax.div(s, lo), lax.rem(s, lo)

    def peer(dx, dy, dc):
        gg = lax.rem(xi + dx, nx) * cores + lax.rem(core + dc, cores)
        yy = lax.rem(y + dy, lo)
        return gg, yy

    def slot(o, dc):
        return dc * count + o

    plane = [(o, dc) for o in range(count) for dc in range(cores) if (o, dc) != (0, 0)]
    plane.sort(key=lambda item: -sum(1 for v in offsets[item[0]] if v))

    barrier = pltpu.get_barrier_semaphore()
    for o, dc in plane:
        gg, yy = peer(*offsets[o], dc)
        pl.semaphore_signal(barrier, inc=1, device_id=(gg, z * lo + yy), device_id_type=MESH)
    for dz in range(1, hi):
        pl.semaphore_signal(
            barrier, inc=1, device_id=(g, lax.rem(z + dz, hi) * lo + y), device_id_type=MESH
        )
    pl.semaphore_wait(barrier, len(plane) + hi - 1)

    def w_columns(c):
        return w_ref.at[:, pl.ds(c * cols, cols)]

    sends = []

    def send_w(c):
        for o in sorted(range(count), key=lambda o: -sum(1 for v in offsets[o] if v)):
            if o == 0:
                if cores > 1:
                    gg, yy = peer(0, 0, 1)
                    k = slot(0, 1)
                else:
                    continue
            else:
                gg, yy = peer(*offsets[o], 0)
                k = slot(o, 0)
            copy = pltpu.make_async_remote_copy(
                src_ref=w_columns(c),
                dst_ref=wbuf.at[c, k],
                send_sem=wsend.at[c, k],
                recv_sem=wrecv.at[c, k],
                device_id=(gg, z * lo + yy),
                device_id_type=MESH,
            )
            copy.start()
            sends.append(copy)

    def relay_w(c):
        if cores == 1:
            return
        gg, yy = peer(0, 0, 1)
        for o in range(1, count):
            wait_w(c, slot(o, 0))
            copy = pltpu.make_async_remote_copy(
                src_ref=wbuf.at[c, slot(o, 0)],
                dst_ref=wbuf.at[c, slot(o, 1)],
                send_sem=wsend.at[c, slot(o, 1)],
                recv_sem=wrecv.at[c, slot(o, 1)],
                device_id=(gg, z * lo + yy),
                device_id_type=MESH,
            )
            copy.start()
            sends.append(copy)

    def wait_w(c, k):
        pltpu.make_async_copy(wbuf.at[c, k], wbuf.at[c, k], wrecv.at[c, k]).wait()

    send_w(0)

    upper = s_ref[...]
    lower = jnp.concatenate([-upper[half:], upper[:half]], axis=0)
    rows_g = hi * lo * block
    contract = (((1,), (1,)), ((), ()))
    for gg in range(plan.grp):
        part = x_ref[pl.ds(gg * rows_g * 2, rows_g * 2), :]
        even_buf[...] = lax.dot_general(part, upper, contract, preferred_element_type=F32)
        odd_buf[...] = lax.dot_general(part, lower, contract, preferred_element_type=F32)
        value = even_buf[pl.ds(0, rows_g, stride=2), :] + odd_buf[pl.ds(1, rows_g, stride=2), :]
        pall[gg] = value.reshape(hi, lo, block, width).astype(BF16)

    for o, dc in plane:
        gg, yy = peer(*offsets[o], dc)
        k = slot(o, dc)
        copy = pltpu.make_async_remote_copy(
            src_ref=pall.at[gg, :, yy],
            dst_ref=pbuf.at[k],
            send_sem=psend.at[k],
            recv_sem=precv.at[k],
            device_id=(gg, z * lo + yy),
            device_id_type=MESH,
        )
        copy.start()
        sends.append(copy)

    for c in range(1, plan.chunks):
        send_w(c)

    for c in range(plan.chunks):
        row = lax.broadcasted_iota(jnp.int32, (cols, plan.beams), 0) + c * cols
        pick_buf[pl.ds(c * cols, cols), :] = jnp.where(row == list_ref[...], 1.0, 0.0).astype(BF16)
        wbuf[c, 0] = w_ref[:, pl.ds(c * cols, cols)]

    lhs_buf[:, pl.ds(0, width)] = pall[g, :, y].reshape(hi * block, width)
    relay_w(0)
    for o, dc in reversed(plane):
        k = slot(o, dc)
        pltpu.make_async_copy(pbuf.at[k], pbuf.at[k], precv.at[k]).wait()
        lhs_buf[:, pl.ds(k * width, width)] = pbuf[k].reshape(hi * block, width)

    def finish(c):
        total = own_buf[c, z]
        for dz in range(1, hi):
            pltpu.make_async_copy(got_buf.at[c, dz], got_buf.at[c, dz], srecv.at[c, dz]).wait()
            total = total + got_buf[c, dz].astype(F32)
        rounded = total.astype(BF16).reshape(2 * block, cols)
        placed = jnp.dot(rounded, pick_buf[pl.ds(c * cols, cols), :], preferred_element_type=F32)
        if c == 0:
            acc_buf[...] = placed
        else:
            acc_buf[...] += placed

    for c in range(plan.chunks):
        if c + 1 < plan.chunks:
            pass
        if cores > 1:
            for o in range(count):
                wait_w(c, slot(o, 1))
        else:
            for o in range(1, count):
                wait_w(c, slot(o, 0))
        weights = wbuf[c]
        w_real, w_imag = weights[:, :half], weights[:, half:]
        for part, rhs in enumerate(((w_real, -w_imag), (w_imag, w_real))):
            rhs = jnp.concatenate(rhs, axis=1).reshape(plan.slots * width, cols)
            value = jnp.dot(lhs_buf[...], rhs, preferred_element_type=F32)
            value = value.reshape(hi, block, cols)
            own_buf[c, :, part] = value
            share_buf[c, :, part] = value.astype(BF16)
        for dz in range(1, hi):
            zz = lax.rem(z + dz, hi)
            copy = pltpu.make_async_remote_copy(
                src_ref=share_buf.at[c, zz],
                dst_ref=got_buf.at[c, dz],
                send_sem=ssend.at[c, dz],
                recv_sem=srecv.at[c, dz],
                device_id=(g, zz * lo + y),
                device_id_type=MESH,
            )
            copy.start()
            sends.append(copy)
        if c + 1 < plan.chunks:
            relay_w(c + 1)
    for c in range(plan.chunks):
        finish(c)
    out_ref[...] = acc_buf[...].astype(BF16).reshape(2, block, plan.beams)
    for copy in sends:
        copy.wait_send()


def shards(plan, snapshots, steering, combining, beam_list):
    snap, _, _, elements = snapshots.shape
    signal = snapshots.reshape(snap * 2, elements)
    steer = jnp.transpose(steering[0], (0, 2, 1)).reshape(plan.width, elements)
    weights = combining.reshape(plan.width, plan.beams)
    rows_g = plan.hi * plan.lo * plan.block
    vmem = pl.BlockSpec(memory_space=pltpu.VMEM)
    dma = pltpu.SemaphoreType.DMA
    return pl.pallas_call(
        functools.partial(beam_kernel, plan),
        out_shape=jax.ShapeDtypeStruct((2, plan.block, plan.beams), BF16),
        in_specs=[vmem] * 4,
        out_specs=vmem,
        scratch_shapes=[
            pltpu.VMEM((rows_g * 2, plan.width), F32),
            pltpu.VMEM((rows_g * 2, plan.width), F32),
            pltpu.VMEM((plan.grp, plan.hi, plan.lo, plan.block, plan.width), BF16),
            pltpu.VMEM((plan.slots, plan.hi, plan.block, plan.width), BF16),
            pltpu.VMEM((plan.hi * plan.block, plan.slots * plan.width), BF16),
            pltpu.VMEM((plan.chunks, plan.slots, plan.width, plan.cols), BF16),
            pltpu.VMEM((plan.chunks, plan.hi, 2, plan.block, plan.cols), F32),
            pltpu.VMEM((plan.chunks, plan.hi, 2, plan.block, plan.cols), BF16),
            pltpu.VMEM((plan.chunks, plan.hi, 2, plan.block, plan.cols), BF16),
            pltpu.VMEM((plan.beams, plan.beams), BF16),
            pltpu.VMEM((2 * plan.block, plan.beams), F32),
            dma((plan.slots,)),
            dma((plan.slots,)),
            dma((plan.chunks, plan.slots)),
            dma((plan.chunks, plan.slots)),
            dma((plan.chunks, plan.hi)),
            dma((plan.chunks, plan.hi)),
        ],
        compiler_params=pltpu.CompilerParams(
            collective_id=0, has_side_effects=True, vmem_limit_bytes=60 * 1024 * 1024
        ),
    )(signal, steer, weights, beam_list.reshape(1, plan.beams))


def solution(mesh):
    placed = (
        P(None, None, ("grp", "sub"), None),
        P(("grp", "sub"), None, None, None),
        P(("grp", "sub"), None, None, None),
        P(),
    )

    def whole(snapshots, steering, combining, beam_list):
        plan = Plan(mesh, snapshots.shape[0], 2 * steering.shape[3], combining.shape[3])
        return jax.shard_map(
            functools.partial(shards, plan),
            mesh=mesh,
            in_specs=placed,
            out_specs=P(None, ("grp", "sub"), None),
            check_vma=False,
        )(snapshots, steering, combining, beam_list)

    return whole
```

time: 126 us -> 44.3 us (0.35)
  the two profiles are of different devices: /device:TPU:0 before, /device:TPU:1 now
where the time goes in v1:
time: 44.3 us; the launch traced here: 44.2 us
  Pallas kernels  42.5 us (96%)
  local copies, waits for them, and re-layouts  1.67 us (4%)
    pallas_call x1, Pallas kernels, shards(): pl.pallas_call(functools.partial(beam_kernel, plan), out_shape=jax.ShapeD...  42.5 us
    unnamed x1, local copies, waits for them, and re-layouts  1.67 us

profile of v1, /device:TPU:1, one launch (start us, length us, event | category | flops | bytes accessed | tf_op | source)
XLA Modules:
  0.0 44.2 jit_solution(5171735587986865504)
XLA Ops:
  0.0 42.5 %shard_map.46 = bf16[2,64,1024]{2,1,0:T(8,128)(2,1)} custom-call(bf16[4096,128]{1,0:T(8,128)(2,1)} %bitcast.8, bf16[128,128]{1,0:T(8,128)(2,1)} %bitcast.10, bf16[128,1024]{1,0:T(8,128)(2,1)} %bitcast.9, s32[1,1024]{1,0:T(1,128)} %bitcast.11), custom_call_target="tpu_custom_call" | custom-call | tf_op jit(solution)/shard_map/pallas_call | solution.py:235
  42.5 1.7 %copy.6 = bf16[2,64,1024]{2,1,0:T(8,128)(2,1)} copy(bf16[2,64,1024]{2,1,0:T(8,128)(2,1)} %shard_map.46) | data formatting | bytes 524288

commit v2 on v1

v2 whole, which is shorter than its diff:
```python
import functools

import jax
import jax.numpy as jnp
from jax import lax
from jax.experimental import pallas as pl
from jax.experimental.pallas import tpu as pltpu
from jax.sharding import PartitionSpec as P

MESH = pl.DeviceIdType.MESH
F32 = jnp.float32
BF16 = jnp.bfloat16
LAG = 2


class Plan:
    def __init__(self, mesh, snap, width, beams):
        self.grp = mesh.shape["grp"]
        self.sub = mesh.shape["sub"]
        self.cores = 2 if self.grp % 2 == 0 else 1
        self.nx = self.grp // self.cores
        self.halves, self.pair = (2, 2) if self.sub % 4 == 0 else (1, 1)
        self.hi = self.halves * self.pair
        self.lo = self.sub // self.hi
        self.block = snap // (self.grp * self.sub)
        self.width = width
        self.beams = beams
        self.chunks = 8 if beams % 1024 == 0 else 1
        self.cols = beams // self.chunks
        self.offsets = [(dx, dy) for dx in range(self.nx) for dy in range(self.lo)]
        self.slots = len(self.offsets) * self.cores


def beam_kernel(
    plan,
    x_hbm,
    s_ref,
    w_hbm,
    list_ref,
    out_ref,
    x_ref,
    w_ref,
    in_sem,
    even_buf,
    odd_buf,
    pall,
    pbuf,
    lhs_buf,
    wbuf,
    own_buf,
    share_buf,
    merged_buf,
    got_buf,
    pick_buf,
    acc_buf,
    psend,
    precv,
    wsend,
    wrecv,
    ssend,
    srecv,
):
    cores, nx, lo, hi = plan.cores, plan.nx, plan.lo, plan.hi
    halves, pair = plan.halves, plan.pair
    cols, width, block = plan.cols, plan.width, plan.block
    half = width // 2
    offsets = plan.offsets
    count = len(offsets)
    g = lax.axis_index("grp")
    s = lax.axis_index("sub")
    core, xi = lax.rem(g, cores), lax.div(g, cores)
    z, y = lax.div(s, lo), lax.rem(s, lo)
    zh, zl = lax.div(z, pair), lax.rem(z, pair)

    def peer(dx, dy, dc):
        gg = lax.rem(xi + dx, nx) * cores + lax.rem(core + dc, cores)
        yy = lax.rem(y + dy, lo)
        return gg, yy

    def slot(o, dc):
        return dc * count + o

    plane = [(o, dc) for o in range(count) for dc in range(cores) if (o, dc) != (0, 0)]
    plane.sort(key=lambda item: -sum(1 for v in offsets[item[0]] if v))

    load_w = pltpu.make_async_copy(w_hbm, w_ref, in_sem.at[0])
    load_w.start()
    load_x = pltpu.make_async_copy(x_hbm, x_ref, in_sem.at[1])
    load_x.start()
    barrier = pltpu.get_barrier_semaphore()
    for o, dc in plane:
        gg, yy = peer(*offsets[o], dc)
        pl.semaphore_signal(barrier, inc=1, device_id=(gg, z * lo + yy), device_id_type=MESH)
    if hi > 1:
        near = (g, (2 * zh + 1 - zl) * lo + y)
        far = (g, (2 * (1 - zh) + zl) * lo + y)
        for target in (near, far):
            pl.semaphore_signal(barrier, inc=1, device_id=target, device_id_type=MESH)
    pl.semaphore_wait(barrier, len(plane) + (2 if hi > 1 else 0))

    def w_columns(c):
        return w_ref.at[:, pl.ds(c * cols, cols)]

    sends = []

    def send_w(c):
        for o in sorted(range(count), key=lambda o: -sum(1 for v in offsets[o] if v)):
            if o == 0:
                if cores > 1:
                    gg, yy = peer(0, 0, 1)
                    k = slot(0, 1)
                else:
                    continue
            else:
                gg, yy = peer(*offsets[o], 0)
                k = slot(o, 0)
            copy = pltpu.make_async_remote_copy(
                src_ref=w_columns(c),
                dst_ref=wbuf.at[c, k],
                send_sem=wsend.at[c, k],
                recv_sem=wrecv.at[c, k],
                device_id=(gg, z * lo + yy),
                device_id_type=MESH,
            )
            copy.start()
            sends.append(copy)

    def relay_w(c):
        if cores == 1:
            return
        gg, yy = peer(0, 0, 1)
        for o in range(1, count):
            wait_w(c, slot(o, 0))
            copy = pltpu.make_async_remote_copy(
                src_ref=wbuf.at[c, slot(o, 0)],
                dst_ref=wbuf.at[c, slot(o, 1)],
                send_sem=wsend.at[c, slot(o, 1)],
                recv_sem=wrecv.at[c, slot(o, 1)],
                device_id=(gg, z * lo + yy),
                device_id_type=MESH,
            )
            copy.start()
            sends.append(copy)

    def wait_w(c, k):
        pltpu.make_async_copy(wbuf.at[c, k], wbuf.at[c, k], wrecv.at[c, k]).wait()

    load_w.wait()
    send_w(0)
    load_x.wait()

    upper = s_ref[...]
    lower = jnp.concatenate([-upper[half:], upper[:half]], axis=0)
    rows_g = hi * lo * block
    contract = (((1,), (1,)), ((), ()))
    for gg in range(plan.grp):
        part = x_ref[pl.ds(gg * rows_g * 2, rows_g * 2), :]
        even_buf[...] = lax.dot_general(part, upper, contract, preferred_element_type=F32)
        odd_buf[...] = lax.dot_general(part, lower, contract, preferred_element_type=F32)
        value = even_buf[pl.ds(0, rows_g, stride=2), :] + odd_buf[pl.ds(1, rows_g, stride=2), :]
        pall[gg] = value.reshape(halves, pair, lo, block, width).astype(BF16)

    def half_of(h):
        return zh if h == halves - 1 else 1 - zh

    def send_p(h):
        for o, dc in plane:
            gg, yy = peer(*offsets[o], dc)
            k = slot(o, dc)
            copy = pltpu.make_async_remote_copy(
                src_ref=pall.at[gg, half_of(h), :, yy],
                dst_ref=pbuf.at[h, k],
                send_sem=psend.at[h, k],
                recv_sem=precv.at[h, k],
                device_id=(gg, z * lo + yy),
                device_id_type=MESH,
            )
            copy.start()
            sends.append(copy)

    def wait_p(h):
        own = pall[g, half_of(h), :, y]
        lhs_buf[h, :, pl.ds(0, width)] = own.reshape(pair * block, width)
        for o, dc in reversed(plane):
            k = slot(o, dc)
            pltpu.make_async_copy(pbuf.at[h, k], pbuf.at[h, k], precv.at[h, k]).wait()
            lhs_buf[h, :, pl.ds(k * width, width)] = pbuf[h, k].reshape(pair * block, width)

    send_p(0)
    for c in range(1, 3):
        send_w(c)

    for c in range(plan.chunks):
        row = lax.broadcasted_iota(jnp.int32, (cols, plan.beams), 0) + c * cols
        pick_buf[pl.ds(c * cols, cols), :] = jnp.where(row == list_ref[...], 1.0, 0.0).astype(BF16)
        wbuf[c, 0] = w_ref[:, pl.ds(c * cols, cols)]

    relay_w(0)
    wait_p(0)

    def share(c, k, source, target):
        copy = pltpu.make_async_remote_copy(
            src_ref=source,
            dst_ref=got_buf.at[c, k],
            send_sem=ssend.at[c, k],
            recv_sem=srecv.at[c, k],
            device_id=target,
            device_id_type=MESH,
        )
        copy.start()
        sends.append(copy)

    def wait_share(c, k):
        pltpu.make_async_copy(got_buf.at[c, k], got_buf.at[c, k], srecv.at[c, k]).wait()

    def merge(c):
        if hi == 1:
            return
        wait_share(c, 0)
        merged_buf[c] = (own_buf[0, c, zl] + got_buf[c, 0].astype(F32)).astype(BF16)
        share(c, 2, merged_buf.at[c], far)

    def finish(c):
        total = own_buf[halves - 1, c, zl]
        if hi > 1:
            for k in (1, 2):
                wait_share(c, k)
                total = total + got_buf[c, k].astype(F32)
        rounded = total.astype(BF16).reshape(2 * block, cols)
        placed = jnp.dot(rounded, pick_buf[pl.ds(c * cols, cols), :], preferred_element_type=F32)
        if c == 0:
            acc_buf[...] = placed
        else:
            acc_buf[...] += placed

    def multiply(h, c):
        weights = wbuf[c]
        w_real, w_imag = weights[:, :half], weights[:, half:]
        for part, rhs in enumerate(((w_real, -w_imag), (w_imag, w_real))):
            rhs = jnp.concatenate(rhs, axis=1).reshape(plan.slots * width, cols)
            value = jnp.dot(lhs_buf[h], rhs, preferred_element_type=F32)
            value = value.reshape(pair, block, cols)
            own_buf[h, c, :, part] = value
            share_buf[h, c, :, part] = value.astype(BF16)
        if hi > 1:
            share(c, h, share_buf.at[h, c, 1 - zl], near)

    for c in range(plan.chunks):
        if c + 3 < plan.chunks:
            send_w(c + 3)
        if c == plan.chunks - 3:
            send_p(1)
        for o in range(count):
            if cores > 1:
                wait_w(c, slot(o, 1))
            elif o > 0:
                wait_w(c, slot(o, 0))
        multiply(0, c)
        if c >= LAG:
            merge(c - LAG)
        if c + 1 < plan.chunks:
            relay_w(c + 1)
    for c in range(max(plan.chunks - LAG, 0), plan.chunks):
        merge(c)
    for h in range(1, halves):
        wait_p(h)
        for c in range(plan.chunks):
            multiply(h, c)
    for c in range(plan.chunks):
        finish(c)
    out_ref[...] = acc_buf[...].astype(BF16).reshape(2, block, plan.beams)
    for copy in sends:
        copy.wait_send()


def shards(plan, snapshots, steering, combining, beam_list):
    snap, _, _, elements = snapshots.shape
    signal = snapshots.reshape(snap * 2, elements)
    steer = jnp.transpose(steering[0], (0, 2, 1)).reshape(plan.width, elements)
    weights = combining.reshape(plan.width, plan.beams)
    rows_g = plan.hi * plan.lo * plan.block
    line = (plan.halves, plan.pair)
    vmem = pl.BlockSpec(memory_space=pltpu.VMEM)
    hbm = pl.BlockSpec(memory_space=pl.ANY)
    dma = pltpu.SemaphoreType.DMA
    return pl.pallas_call(
        functools.partial(beam_kernel, plan),
        out_shape=jax.ShapeDtypeStruct((2, plan.block, plan.beams), BF16),
        in_specs=[hbm, vmem, hbm, vmem],
        out_specs=vmem,
        scratch_shapes=[
            pltpu.VMEM(signal.shape, BF16),
            pltpu.VMEM(weights.shape, BF16),
            dma((2,)),
            pltpu.VMEM((rows_g * 2, plan.width), F32),
            pltpu.VMEM((rows_g * 2, plan.width), F32),
            pltpu.VMEM((plan.grp, *line, plan.lo, plan.block, plan.width), BF16),
            pltpu.VMEM((plan.halves, plan.slots, plan.pair, plan.block, plan.width), BF16),
            pltpu.VMEM((plan.halves, plan.pair * plan.block, plan.slots * plan.width), BF16),
            pltpu.VMEM((plan.chunks, plan.slots, plan.width, plan.cols), BF16),
            pltpu.VMEM((plan.halves, plan.chunks, plan.pair, 2, plan.block, plan.cols), F32),
            pltpu.VMEM((plan.halves, plan.chunks, plan.pair, 2, plan.block, plan.cols), BF16),
            pltpu.VMEM((plan.chunks, 2, plan.block, plan.cols), BF16),
            pltpu.VMEM((plan.chunks, 3, 2, plan.block, plan.cols), BF16),
            pltpu.VMEM((plan.beams, plan.beams), BF16),
            pltpu.VMEM((2 * plan.block, plan.beams), F32),
            dma((plan.halves, plan.slots)),
            dma((plan.halves, plan.slots)),
            dma((plan.chunks, plan.slots)),
            dma((plan.chunks, plan.slots)),
            dma((plan.chunks, 3)),
            dma((plan.chunks, 3)),
        ],
        compiler_params=pltpu.CompilerParams(
            collective_id=0, has_side_effects=True, vmem_limit_bytes=60 * 1024 * 1024
        ),
    )(signal, steer, weights, beam_list.reshape(1, plan.beams))


def solution(mesh):
    placed = (
        P(None, None, ("grp", "sub"), None),
        P(("grp", "sub"), None, None, None),
        P(("grp", "sub"), None, None, None),
        P(),
    )

    def whole(snapshots, steering, combining, beam_list):
        plan = Plan(mesh, snapshots.shape[0], 2 * steering.shape[3], combining.shape[3])
        return jax.shard_map(
            functools.partial(shards, plan),
            mesh=mesh,
            in_specs=placed,
            out_specs=P(None, ("grp", "sub"), None),
            check_vma=False,
        )(snapshots, steering, combining, beam_list)

    return whole
```

time: 44.3 us -> 40.8 us (0.921)
  the two profiles are of different devices: /device:TPU:1 before, /device:TPU:0 now
where the time goes in v2:
time: 40.8 us; the launch traced here: 40.6 us
  Pallas kernels  38.9 us (95%)
  local copies, waits for them, and re-layouts  1.67 us (4%)
    pallas_call x1, Pallas kernels, shards(): pl.pallas_call(functools.partial(beam_kernel, plan), out_shape=jax.ShapeD...  38.9 us
    unnamed x1, local copies, waits for them, and re-layouts  1.67 us

profile of v2, /device:TPU:0, one launch (start us, length us, event | category | flops | bytes accessed | tf_op | source)
XLA Modules:
  0.0 40.6 jit_solution(13503642096918597906)
XLA Ops:
  0.0 38.9 %shard_map.46 = bf16[2,64,1024]{2,1,0:T(8,128)(2,1)} custom-call(bf16[4096,128]{1,0:T(8,128)(2,1)} %bitcast.8, bf16[128,128]{1,0:T(8,128)(2,1)} %bitcast.10, bf16[128,1024]{1,0:T(8,128)(2,1)} %bitcast.9, s32[1,1024]{1,0:T(1,128)} %bitcast.11), custom_call_target="tpu_custom_call" | custom-call | tf_op jit(solution)/shard_map/pallas_call | solution.py:286
  38.9 1.7 %copy.6 = bf16[2,64,1024]{2,1,0:T(8,128)(2,1)} copy(bf16[2,64,1024]{2,1,0:T(8,128)(2,1)} %shard_map.46) | data formatting | bytes 524288
